TPU v7x, 32 devices: a whole 2x2x4 slice. The times are simulated.
32 devices in a mesh: rows: 8 (over z, x), cols: 4 (over y, core).
Axes of the slice: x: 2, y: 2, z: 4, core: 2. Of those that a mesh axis runs over, the one named last changes fastest.
Arguments:
- matrix: float32 [512, 32, 2, 128], P('rows', 'cols'), may hold values from -54 to 54
- plan: int32 [2, 4, 256], replicated, may hold values from 0 to 255, as said below
Outputs:
- rotated: float32 [512, 32, 2, 128], P('rows', 'cols')
Inputs may be any that keep to these rules, and one draw needn't show every extreme that they name: Each plan[s, r] pairs the 256 columns: partner of partner of i is i, and no column is its own partner.
All inputs are finite; a program needn't handle non-finite values.
Results may differ from a plain program's by a relative error of at most 0.0003.
Values sent between devices are 32-bit elements; how exact they have to be, the bound alone decides.
A program may use at most 128 MiB of HBM per device.

v0:
```python
import jax
import jax.numpy as jnp
from jax import lax
from jax.sharding import PartitionSpec as P

STEPS = 2


def passed_along(block, axis, distance):
    devices = range(lax.axis_size(axis))
    route = [((i - distance) % len(devices), i) for i in devices]
    return lax.ppermute(block, axis, route)


def diagonalize(grams, table):
    width = grams.shape[1]
    indices = jnp.arange(width, dtype=jnp.int32)
    rotation = jnp.broadcast_to(jnp.eye(width, dtype=jnp.float32), grams.shape)
    unit_matrix = jnp.eye(width, dtype=jnp.float32)
    for round_index in range(table.shape[0]):
        partner = table[round_index]
        onehot = (partner[:, None] == indices[None, :]).astype(jnp.float32)
        diagonal_now = jnp.diagonal(grams, axis1=1, axis2=2)
        partner_diag = jnp.einsum(
            "pj,ij->pi", diagonal_now, onehot, precision=lax.Precision.HIGHEST
        )
        partner_gram = jnp.sum(grams * onehot[None], axis=2)
        orient = jnp.where(indices < partner, 1.0, -1.0).astype(jnp.float32)
        spread = orient[None, :] * (partner_diag - diagonal_now)
        sign_part = jnp.where(spread >= 0.0, 1.0, -1.0).astype(jnp.float32)
        tangent = (
            sign_part
            * 2.0
            * partner_gram
            / (jnp.abs(spread) + jnp.sqrt(spread * spread + 4.0 * partner_gram * partner_gram))
        )
        cosine = 1.0 / jnp.sqrt(1.0 + tangent * tangent)
        sine_part = tangent * cosine
        off_part = jnp.swapaxes(onehot[None] * (-orient[None, :] * sine_part)[:, :, None], 1, 2)
        rot_now = cosine[:, :, None] * unit_matrix[None] + off_part
        product = jnp.einsum("pij,pjk->pik", grams, rot_now, precision=lax.Precision.HIGHEST)
        grams = jnp.einsum("pji,pjk->pik", rot_now, product, precision=lax.Precision.HIGHEST)
        rotation = jnp.einsum("pij,pjk->pik", rotation, rot_now, precision=lax.Precision.HIGHEST)
    return (grams, rotation)


def full_grams(columns):
    local_sum = jnp.einsum("mpi,mpj->pij", columns, columns, precision=lax.Precision.HIGHEST)
    return lax.psum(local_sum, "rows")


def body(matrix, plan):
    rows_here, pair_here, halves, width = matrix.shape
    columns = matrix.reshape(rows_here, pair_here, halves * width)
    grams = full_grams(columns)
    for step_index in range(STEPS):
        grams, rotation = diagonalize(grams, plan[step_index])
        columns = jnp.einsum("mpi,pij->mpj", columns, rotation, precision=lax.Precision.HIGHEST)
        quarter = columns.reshape(rows_here, pair_here, halves, width)
        tops = quarter[:, :, 0, :]
        bottoms = quarter[:, :, 1, :]
        bottoms, low_grams = passed_along((bottoms, grams[:, width:, width:]), "cols", 1)
        columns = jnp.stack([tops, bottoms], axis=2).reshape(rows_here, pair_here, halves * width)
        if step_index + 1 < STEPS:
            cross_local = jnp.einsum("mpi,mpj->pij", tops, bottoms, precision=lax.Precision.HIGHEST)
            cross = lax.psum(cross_local, "rows")
            upper_rows = jnp.concatenate([grams[:, :width, :width], cross], axis=2)
            lower_rows = jnp.concatenate([jnp.swapaxes(cross, 1, 2), low_grams], axis=2)
            grams = jnp.concatenate([upper_rows, lower_rows], axis=1)
    return columns.reshape(matrix.shape)


def solution(mesh):
    in_specs = (P("rows", "cols", None, None), P())
    out_specs = P("rows", "cols", None, None)
    return jax.shard_map(body, mesh=mesh, in_specs=in_specs, out_specs=out_specs, check_vma=False)
```

profile of v0, /device:TPU:0, one launch (start us, length us, event | category | flops | bytes accessed | tf_op | source)
XLA Modules:
  0.0 463.2 jit_solution(2592383849989567668)
XLA Ops:
  8.0 3.2 fusion.123
  24.4 92.0 %all-reduce.3.cloned.1.call-done = f32[8,256,256]{2,1,0:T(8,128)} async-done(((f32[8,256,256]{2,1,0:T(8,128)}), f32[8,256,256]{2,1,0:T(8,128)}) %all-reduce.3.cloned.1.call-update) | async-done | bytes 2097168 | tf_op jit(solution)/shard_map/psum | solution.py:49
  116.4 17.5 %copy.30 = f32[8,256,256]{0,2,1:T(8,128)} copy(f32[8,256,256]{2,1,0:T(8,128)} %all-reduce.3.cloned.1.call-done) | data formatting | bytes 4194304 | tf_op jit(solution)/shard_map/psum | solution.py:49
  133.9 2.3 gather_fusion
  138.7 3.5 fusion.22
  142.2 4.1 fusion.24
  146.3 3.3 multiply_reduce_fusion.6
  149.6 16.5 %copy.32 = f32[8,256,256]{0,2,1:T(8,128)} copy(f32[8,256,256]{1,2,0:T(8,128)S(1)} %get-tuple-element.56) | data formatting | bytes 4194304 | tf_op jit(solution)/shard_map/pji,pjk->pik/dot_general | solution.py:42
  166.1 2.3 gather_fusion.1
  170.1 5.1 %fusion.21 = f32[8,256,256]{1,2,0:T(8,128)S(1)} fusion(f32[8,256,256]{1,2,0:T(8,128)S(1)} %get-tuple-element.56, f32[8,256]{1,0:T(8,128)S(1)} %get-tuple-element.34, f32[256,256]{1,0:T(8,128)} %fusion.135, f32[8,256]{1,0:T(8,128)S(1)} %get-tuple-element.33, f32[256,256]{1,0:T(8,128)S(1)} %get-tuple-element.67), kind=kOutput, calls=%fused_computation.42 | convolution fusion | flops 1612185600 | bytes 4734976 | tf_op jit(solution)/shard_map/pij,pjk->pik/dot_general | solution.py:41
  175.2 3.3 multiply_reduce_fusion.5
  178.6 16.6 %copy.34 = f32[8,256,256]{0,2,1:T(8,128)} copy(f32[8,256,256]{1,2,0:T(8,128)S(1)} %get-tuple-element.58) | data formatting | bytes 4194304 | tf_op jit(solution)/shard_map/pji,pjk->pik/dot_general | solution.py:42
  195.2 2.3 gather_fusion.2
  199.3 5.1 %fusion.18 = f32[8,256,256]{1,2,0:T(8,128)S(1)} fusion(f32[8,256,256]{1,2,0:T(8,128)S(1)} %get-tuple-element.58, f32[8,256]{1,0:T(8,128)S(1)} %get-tuple-element.32, f32[256,256]{1,0:T(8,128)} %fusion.136, f32[8,256]{1,0:T(8,128)S(1)} %get-tuple-element.31, f32[256,256]{1,0:T(8,128)S(1)} %get-tuple-element.67), kind=kOutput, calls=%fused_computation.37 | convolution fusion | flops 1612185600 | bytes 4734976 | tf_op jit(solution)/shard_map/pij,pjk->pik/dot_general | solution.py:41
  204.4 3.3 multiply_reduce_fusion.4
  207.8 16.4 %copy.36 = f32[8,256,256]{0,2,1:T(8,128)} copy(f32[8,256,256]{1,2,0:T(8,128)S(1)} %get-tuple-element.60) | data formatting | bytes 4194304 | tf_op jit(solution)/shard_map/pji,pjk->pik/dot_general | solution.py:42
  224.2 2.3 gather_fusion.3
  228.2 5.1 %fusion.15 = f32[8,256,256]{1,2,0:T(8,128)S(1)} fusion(f32[8,256,256]{1,2,0:T(8,128)S(1)} %get-tuple-element.60, f32[8,256]{1,0:T(8,128)S(1)} %get-tuple-element.30, f32[256,256]{1,0:T(8,128)} %fusion.137, f32[8,256]{1,0:T(8,128)S(1)} %get-tuple-element.29, f32[256,256]{1,0:T(8,128)S(1)} %get-tuple-element.67), kind=kOutput, calls=%fused_computation.32 | convolution fusion | flops 1612185600 | bytes 4734976 | tf_op jit(solution)/shard_map/pij,pjk->pik/dot_general | solution.py:41
  233.3 2.6 fusion.14
  236.0 2.5 fusion.19
  238.5 2.7 fusion.16
  241.3 2.5 fusion.13
  243.8 2.4 convolution_bitcast_fusion.1
  246.2 2.1 reshape.365
  248.3 1.7 fusion.192
  252.7 3.1 collective-permute-done
  255.8 1.8 fusion.194
  259.6 70.2 %all-reduce.5.cloned.1.call-done = f32[8,128,128]{1,2,0:T(8,128)} async-done(((f32[8,128,128]{1,2,0:T(8,128)}), f32[8,128,128]{1,2,0:T(8,128)}) %all-reduce.5.cloned.1.call-update) | async-done | bytes 524304 | tf_op jit(solution)/shard_map/psum | solution.py:66
  331.9 1.7 maximum_maximum_fusion
  333.6 16.7 %copy.43 = f32[8,256,256]{0,2,1:T(8,128)} copy(f32[8,256,256]{1,2,0:T(8,128)S(1)} %get-tuple-element.5) | data formatting | bytes 4194304 | tf_op jit(solution)/shard_map/concatenate | solution.py:69
  350.3 2.4 gather_fusion.4
  353.1 3.5 fusion.12
  356.6 4.1 fusion.11
  360.7 2.7 multiply_reduce_fusion.2
  363.5 16.4 %copy.45 = f32[8,256,256]{0,2,1:T(8,128)} copy(f32[8,256,256]{1,2,0:T(8,128)S(1)} %get-tuple-element.62) | data formatting | bytes 4194304 | tf_op jit(solution)/shard_map/pji,pjk->pik/dot_general | solution.py:42
  380.0 2.3 gather_fusion.5
  382.6 4.1 fusion.8
  386.8 3.8 fusion.9
  390.5 2.7 multiply_reduce_fusion.1
  393.3 16.5 %copy.47 = f32[8,256,256]{0,2,1:T(8,128)} copy(f32[8,256,256]{1,2,0:T(8,128)S(1)} %get-tuple-element.64) | data formatting | bytes 4194304 | tf_op jit(solution)/shard_map/pji,pjk->pik/dot_general | solution.py:42
  409.8 2.3 gather_fusion.6
  412.5 4.1 fusion.5
  416.6 3.8 fusion.6
  420.4 2.7 multiply_reduce_fusion
  423.1 16.5 %copy.49 = f32[8,256,256]{0,2,1:T(8,128)} copy(f32[8,256,256]{1,2,0:T(8,128)S(1)} %get-tuple-element.66) | data formatting | bytes 4194304 | tf_op jit(solution)/shard_map/pji,pjk->pik/dot_general | solution.py:42
  439.6 2.3 gather_fusion.7
  442.3 4.1 fusion
  449.0 5.8 %collective-permute-done.2 = f32[64,8,128]{2,1,0:T(8,128)S(1)} collective-permute-done((f32[64,8,128]{2,1,0:T(8,128)S(1)}, f32[64,8,128]{2,1,0:T(8,128)S(1)}, u32[]{:S(2)}, u32[]{:S(2)}) %collective-permute-start.2) | collective-permute-done | bytes 262176 | tf_op jit(solution)/shard_map/ppermute | solution.py:12
  (156 shorter events, 34.0 us)
Async XLA Ops:
  6.5 109.9 %all-reduce.3.cloned.1.call-start = ((), (), s32[]{:S(2)}) async-start(), calls=%async_computation | async-start | bytes 4194304 | tf_op jit(solution)/shard_map/psum | solution.py:49
  8.0 3.5 copy-start.41
  11.2 318.5 %all-reduce.5.cloned.1.call-start = ((), (), s32[]{:S(2)}) async-start(), calls=%async_computation.1 | async-start | bytes 1048576 | tf_op jit(solution)/shard_map/psum | solution.py:66
  11.5 12.9 %copy-start.31 = (s32[1,1,256]{2,1,0:T(1,128)}, s32[1,1,256]{2,1,0:T(1,128)S(1)}, u32[]{:S(2)}) copy-start(s32[1,1,256]{2,1,0:T(1,128)S(1)} %get-tuple-element.22) | copy-start | bytes 3076
  11.5 12.9 %copy-start.33 = (s32[1,1,256]{2,1,0:T(1,128)}, s32[1,1,256]{2,1,0:T(1,128)S(1)}, u32[]{:S(2)}) copy-start(s32[1,1,256]{2,1,0:T(1,128)S(1)} %get-tuple-element.16) | copy-start | bytes 3076
  11.5 12.9 %copy-start.35 = (s32[1,1,256]{2,1,0:T(1,128)}, s32[1,1,256]{2,1,0:T(1,128)S(1)}, u32[]{:S(2)}) copy-start(s32[1,1,256]{2,1,0:T(1,128)S(1)} %get-tuple-element.21) | copy-start | bytes 3076
  11.5 12.9 %copy-start.37 = (s32[1,1,256]{2,1,0:T(1,128)}, s32[1,1,256]{2,1,0:T(1,128)S(1)}, u32[]{:S(2)}) copy-start(s32[1,1,256]{2,1,0:T(1,128)S(1)} %get-tuple-element.20) | copy-start | bytes 3076
  11.5 12.9 %copy-start.38 = (s32[1,1,256]{2,1,0:T(1,128)}, s32[1,1,256]{2,1,0:T(1,128)S(1)}, u32[]{:S(2)}) copy-start(s32[1,1,256]{2,1,0:T(1,128)S(1)} %get-tuple-element.19) | copy-start | bytes 3076
  11.5 12.9 %copy-start.39 = (s32[1,1,256]{2,1,0:T(1,128)}, s32[1,1,256]{2,1,0:T(1,128)S(1)}, u32[]{:S(2)}) copy-start(s32[1,1,256]{2,1,0:T(1,128)S(1)} %get-tuple-element.18) | copy-start | bytes 3076
  11.6 12.9 %copy-start.40 = (s32[1,1,256]{2,1,0:T(1,128)}, s32[1,1,256]{2,1,0:T(1,128)S(1)}, u32[]{:S(2)}) copy-start(s32[1,1,256]{2,1,0:T(1,128)S(1)} %get-tuple-element.17) | copy-start | bytes 3076
  116.4 19.9 %copy-start = (f32[8,256,256]{2,1,0:T(8,128)S(1)}, f32[8,256,256]{2,1,0:T(8,128)}, u32[]{:S(2)}) copy-start(f32[8,256,256]{2,1,0:T(8,128)} %all-reduce.3.cloned.1.call-done) | copy-start | bytes 6291460
  142.2 4.1 copy-start.22
  170.1 5.1 %copy-start.25 = (f32[8,256]{1,0:T(8,128)}, f32[8,256]{1,0:T(8,128)S(1)}, u32[]{:S(2)}) copy-start(f32[8,256]{1,0:T(8,128)S(1)} %get-tuple-element.34) | copy-start | bytes 24580
  170.1 5.1 %copy-start.4 = (f32[256,256]{1,0:T(8,128)S(1)}, f32[256,256]{1,0:T(8,128)}, u32[]{:S(2)}) copy-start(f32[256,256]{1,0:T(8,128)} %fusion.135) | copy-start | bytes 786436
  170.1 5.1 %copy-start.21 = (f32[256,256]{0,1:T(8,128)S(1)}, f32[256,256]{0,1:T(8,128)}, u32[]{:S(2)}) copy-start(f32[256,256]{0,1:T(8,128)} %fusion.130) | copy-start | bytes 786436
  199.2 5.2 %copy-start.27 = (f32[8,256]{1,0:T(8,128)}, f32[8,256]{1,0:T(8,128)S(1)}, u32[]{:S(2)}) copy-start(f32[8,256]{1,0:T(8,128)S(1)} %get-tuple-element.31) | copy-start | bytes 24580
  199.2 5.2 %copy-start.29 = (f32[8,256]{1,0:T(8,128)}, f32[8,256]{1,0:T(8,128)S(1)}, u32[]{:S(2)}) copy-start(f32[8,256]{1,0:T(8,128)S(1)} %get-tuple-element.32) | copy-start | bytes 24580
  199.2 5.2 %copy-start.6 = (f32[256,256]{1,0:T(8,128)S(1)}, f32[256,256]{1,0:T(8,128)}, u32[]{:S(2)}) copy-start(f32[256,256]{1,0:T(8,128)} %fusion.136) | copy-start | bytes 786436
  199.3 5.2 %copy-start.20 = (f32[256,256]{0,1:T(8,128)S(1)}, f32[256,256]{0,1:T(8,128)}, u32[]{:S(2)}) copy-start(f32[256,256]{0,1:T(8,128)} %fusion.129) | copy-start | bytes 786436
  228.2 5.1 %copy-start.8 = (f32[256,256]{1,0:T(8,128)S(1)}, f32[256,256]{1,0:T(8,128)}, u32[]{:S(2)}) copy-start(f32[256,256]{1,0:T(8,128)} %fusion.137) | copy-start | bytes 786436
  233.3 2.6 copy-start.1
  233.3 2.6 copy-start.5
  233.3 2.6 copy-start.26
  250.0 5.8 %collective-permute-start = (f32[64,8,128]{2,0,1:T(8,128)S(1)}, f32[64,8,128]{2,0,1:T(8,128)S(1)}, u32[]{:S(2)}, u32[]{:S(2)}) collective-permute-start(f32[64,8,128]{2,0,1:T(8,128)S(1)} %bitcast.109), channel_id=1, source_target_pairs={{3,0},{0,1},{1,2},{2,3},{7,4},{4,5},{5,6},{6,7},{11,8},{8,9},{9,10... | collective-permute-start | bytes 786440 | tf_op jit(solution)/shard_map/ppermute | solution.py:12
  251.1 79.9 %collective-permute-start.1 = (f32[8,128,128]{1,2,0:T(8,128)}, f32[8,128,128]{1,2,0:T(8,128)S(1)}, u32[]{:S(2)}, u32[]{:S(2)}) collective-permute-start(f32[8,128,128]{1,2,0:T(8,128)} %get-tuple-element.8), channel_id=1, source_target_pairs={{3,0},{0,1},{1,2},{2,3},{7,4},{4,5},{5,6},{6,7},{11,8},{8,9},{9,10... | collective-permute-start | bytes 1572872 | tf_op jit(solution)/shard_map/ppermute | solution.py:12
  331.0 2.6 copy-start.12
  333.6 19.2 %copy-start.36 = (s32[1,1,256]{2,1,0:T(1,128)S(1)}, s32[1,1,256]{2,1,0:T(1,128)}, u32[]{:S(2)}) copy-start(s32[1,1,256]{2,1,0:T(1,128)} %copy-done.35) | copy-start | bytes 3076
  333.6 19.2 %copy-start.46 = (f32[256]{0:T(256)S(1)}, f32[256]{0:T(256)}, u32[]{:S(2)}) copy-start(f32[256]{0:T(256)} %get-tuple-element.43) | copy-start | bytes 3076
  333.6 19.2 %copy-start.47 = (f32[256]{0:T(256)S(1)}, f32[256]{0:T(256)}, u32[]{:S(2)}) copy-start(f32[256]{0:T(256)} %get-tuple-element.44) | copy-start | bytes 3076
  333.6 19.5 %copy-start.10 = (f32[256,256]{1,0:T(8,128)S(1)}, f32[256,256]{1,0:T(8,128)}, u32[]{:S(2)}) copy-start(f32[256,256]{1,0:T(8,128)} %fusion.138) | copy-start | bytes 786436
  350.3 6.2 %copy-start.11 = (f32[8,128,128]{1,2,0:T(8,128)S(1)}, f32[8,128,128]{1,2,0:T(8,128)}, u32[]{:S(2)}) copy-start(f32[8,128,128]{1,2,0:T(8,128)} %all-reduce.5.cloned.1.call-done) | copy-start | bytes 1572868
  350.3 6.2 %copy-start.13 = (f32[8,128,128]{1,2,0:T(8,128)S(1)}, f32[8,128,128]{1,2,0:T(8,128)}, u32[]{:S(2)}) copy-start(f32[8,128,128]{1,2,0:T(8,128)} %copy-done.12) | copy-start | bytes 1572868
  350.3 6.2 %copy-start.14 = (f32[8,128,128]{1,2,0:T(8,128)S(1)}, f32[8,128,128]{1,2,0:T(8,128)}, u32[]{:S(2)}) copy-start(f32[8,128,128]{1,2,0:T(8,128)} %get-tuple-element.7) | copy-start | bytes 1572868
  350.3 6.2 %copy-start.24 = (f32[8,128,128]{1,2,0:T(8,128)S(1)}, f32[8,128,128]{1,2,0:T(8,128)}, u32[]{:S(2)}) copy-start(f32[8,128,128]{1,2,0:T(8,128)} %copy-done.23) | copy-start | bytes 1572868
  356.6 4.1 copy-start.18
  363.5 18.9 %copy-start.34 = (s32[1,1,256]{2,1,0:T(1,128)S(1)}, s32[1,1,256]{2,1,0:T(1,128)}, u32[]{:S(2)}) copy-start(s32[1,1,256]{2,1,0:T(1,128)} %copy-done.33) | copy-start | bytes 3076
  363.5 18.9 %copy-start.44 = (f32[256]{0:T(256)S(1)}, f32[256]{0:T(256)}, u32[]{:S(2)}) copy-start(f32[256]{0:T(256)} %get-tuple-element.41) | copy-start | bytes 3076
  363.5 18.8 %copy-start.45 = (f32[256]{0:T(256)S(1)}, f32[256]{0:T(256)}, u32[]{:S(2)}) copy-start(f32[256]{0:T(256)} %get-tuple-element.42) | copy-start | bytes 3076
  382.6 4.1 copy-start.2
  386.8 3.8 copy-start.17
  393.3 18.9 %copy-start.32 = (s32[1,1,256]{2,1,0:T(1,128)S(1)}, s32[1,1,256]{2,1,0:T(1,128)}, u32[]{:S(2)}) copy-start(s32[1,1,256]{2,1,0:T(1,128)} %copy-done.31) | copy-start | bytes 3076
  393.3 18.9 %copy-start.42 = (f32[256]{0:T(256)S(1)}, f32[256]{0:T(256)}, u32[]{:S(2)}) copy-start(f32[256]{0:T(256)} %get-tuple-element.39) | copy-start | bytes 3076
  393.3 18.9 %copy-start.43 = (f32[256]{0:T(256)S(1)}, f32[256]{0:T(256)}, u32[]{:S(2)}) copy-start(f32[256]{0:T(256)} %get-tuple-element.40) | copy-start | bytes 3076
  412.5 4.1 copy-start.3
  416.6 3.8 copy-start.16
  423.1 19.2 %copy-start.19 = (f32[256,256]{1,0:T(8,128)S(1)}, f32[256,256]{1,0:T(8,128)}, u32[]{:S(2)}) copy-start(f32[256,256]{1,0:T(8,128)} %fusion.141) | copy-start | bytes 786436
  442.3 4.2 copy-start.15
  449.0 5.8 %collective-permute-start.2 = (f32[64,8,128]{2,1,0:T(8,128)S(1)}, f32[64,8,128]{2,1,0:T(8,128)S(1)}, u32[]{:S(2)}, u32[]{:S(2)}) collective-permute-start(f32[64,8,128]{2,1,0:T(8,128)S(1)} %bitcast.108), channel_id=1, source_target_pairs={{3,0},{0,1},{1,2},{2,3},{7,4},{4,5},{5,6},{6,7},{11,8},{8,9},{9,10... | collective-permute-start | bytes 786440 | tf_op jit(solution)/shard_map/ppermute | solution.py:12
  (5 other events, 10.9 us)
Sparse Core Ops, SparseCore 0:
  11.4 105.0 all-reduce.2
  257.8 71.9 all-reduce.4
where the time goes:
time: 467 us; the launch traced here: 463 us
  waiting for transfers between devices  171 us (37%)
  local copies, waits for them, and re-layouts  165 us (35%)
  matrix products  92.9 us (20%)
  other arithmetic  18 us (4%)
  between operations  14.6 us (3%)
    dot_general x6, local copies, waits for them, and re-layouts, diagonalize(): jnp.einsum('pji,pjk->pik', rot_now, product, precision=lax.Precision.HIGH...  98.9 us
    psum x1, waiting for transfers between devices, full_grams(): return lax.psum(local_sum, 'rows')  92 us
    psum x1, waiting for transfers between devices, body(): cross = lax.psum(cross_local, 'rows')  70.2 us
    dot_general x7, matrix products, diagonalize(): jnp.einsum('pij,pjk->pik', grams, rot_now, precision=lax.Precision.HIGHEST)  31.7 us
    dot_general x8, matrix products, diagonalize(): jnp.einsum('pij,pjk->pik', rotation, rot_now, precision=lax.Precision.HIG...  26.3 us
    gather x16, local copies, waits for them, and re-layouts, diagonalize(): diagonal_now = jnp.diagonal(grams, axis1=1, axis2=2)  21 us
    dot_general x7, matrix products, diagonalize(): jnp.einsum('pji,pjk->pik', rot_now, product, precision=lax.Precision.HIGH...  20.8 us
    psum x1, local copies, waits for them, and re-layouts, full_grams(): return lax.psum(local_sum, 'rows')  17.5 us
  transfers between devices with their start and end apart: 5, of which 4 were waited for; matrix products, arithmetic and copies ran while one was open for 4% of the time, Pallas kernels for 0%

commit v1 on v0

--- a/solution.py
+++ b/solution.py
@@ -63,7 +63,13 @@
         columns = jnp.stack([tops, bottoms], axis=2).reshape(rows_here, pair_here, halves * width)
         if step_index + 1 < STEPS:
             cross_local = jnp.einsum("mpi,mpj->pij", tops, bottoms, precision=lax.Precision.HIGHEST)
-            cross = lax.psum(cross_local, "rows")
+            peers = lax.axis_size("rows")
+            cross, reach = (cross_local, 1)
+            while reach < peers:
+                cross = cross + lax.ppermute(
+                    cross, "rows", [(i_2, i_2 ^ reach) for i_2 in range(peers)]
+                )
+                reach = 2 * reach
             upper_rows = jnp.concatenate([grams[:, :width, :width], cross], axis=2)
             lower_rows = jnp.concatenate([jnp.swapaxes(cross, 1, 2), low_grams], axis=2)
             grams = jnp.concatenate([upper_rows, lower_rows], axis=1)

time: 467 us -> 438 us (0.938)
  waiting for transfers between devices: 171 us -> 139 us
    psum x1 -> x0, waiting for transfers between devices: 70.2 us -> none  [body(): cross = lax.psum(cross_local, 'rows')]
    ppermute x0 -> x3, waiting for transfers between devices: none -> 34.2 us  [body(): lax.ppermute(cross, 'rows', [(i_2, i_2 ^ reach) for i_2 in range(peers)])]
  transfers between devices with their start and end apart: 5 -> 7, of which waited for: 4 -> 6; matrix products, arithmetic and copies ran while one was open for 4% -> 5% of each run, Pallas kernels for 0% -> 0%
where the time goes in v1:
time: 438 us; the launch traced here: 435 us
  local copies, waits for them, and re-layouts  166 us (38%)
  waiting for transfers between devices  139 us (32%)
  matrix products  92.6 us (21%)
  other arithmetic  17.1 us (4%)
  between operations  14.6 us (3%)
  starting transfers between devices  5.2 us (1%)
    dot_general x6, local copies, waits for them, and re-layouts, diagonalize(): jnp.einsum('pji,pjk->pik', rot_now, product, precision=lax.Precision.HIGH...  101 us
    psum x1, waiting for transfers between devices, full_grams(): return lax.psum(local_sum, 'rows')  94.1 us
    ppermute x3, waiting for transfers between devices, body(): lax.ppermute(cross, 'rows', [(i_2, i_2 ^ reach) for i_2 in range(peers)])  34.2 us
    dot_general x7, matrix products, diagonalize(): jnp.einsum('pij,pjk->pik', grams, rot_now, precision=lax.Precision.HIGHEST)  30.7 us
    dot_general x8, matrix products, diagonalize(): jnp.einsum('pij,pjk->pik', rotation, rot_now, precision=lax.Precision.HIG...  28.6 us
    gather x16, local copies, waits for them, and re-layouts, diagonalize(): diagonal_now = jnp.diagonal(grams, axis1=1, axis2=2)  20.9 us
    dot_general x7, matrix products, diagonalize(): jnp.einsum('pji,pjk->pik', rot_now, product, precision=lax.Precision.HIGH...  20.8 us
    psum x1, local copies, waits for them, and re-layouts, full_grams(): return lax.psum(local_sum, 'rows')  17.7 us
  transfers between devices with their start and end apart: 7, of which 6 were waited for; matrix products, arithmetic and copies ran while one was open for 5% of the time, Pallas kernels for 0%

profile of v1, /device:TPU:0, one launch (start us, length us, event | category | flops | bytes accessed | tf_op | source)
XLA Modules:
  0.0 434.6 jit_solution(7016972761893894517)
XLA Ops:
  8.0 3.2 fusion.123
  22.4 94.1 %all-reduce.2.cloned.1.call-done = f32[8,256,256]{2,1,0:T(8,128)} async-done(((f32[8,256,256]{2,1,0:T(8,128)}), f32[8,256,256]{2,1,0:T(8,128)}) %all-reduce.2.cloned.1.call-update) | async-done | bytes 2097168 | tf_op jit(solution)/shard_map/psum | solution.py:49
  116.5 17.7 %copy.31 = f32[8,256,256]{0,2,1:T(8,128)} copy(f32[8,256,256]{2,1,0:T(8,128)} %all-reduce.2.cloned.1.call-done) | data formatting | bytes 4194304 | tf_op jit(solution)/shard_map/psum | solution.py:49
  134.2 2.3 gather_fusion
  139.0 3.5 fusion.22
  142.5 4.1 fusion.24
  146.5 3.3 multiply_reduce_fusion.6
  149.9 16.7 %copy.33 = f32[8,256,256]{0,2,1:T(8,128)} copy(f32[8,256,256]{1,2,0:T(8,128)S(1)} %get-tuple-element.56) | data formatting | bytes 4194304 | tf_op jit(solution)/shard_map/pji,pjk->pik/dot_general | solution.py:42
  166.6 2.3 gather_fusion.1
  170.6 5.1 %fusion.21 = f32[8,256,256]{1,2,0:T(8,128)S(1)} fusion(f32[8,256,256]{1,2,0:T(8,128)S(1)} %get-tuple-element.56, f32[8,256]{1,0:T(8,128)S(1)} %get-tuple-element.34, f32[256,256]{1,0:T(8,128)} %fusion.135, f32[8,256]{1,0:T(8,128)S(1)} %get-tuple-element.33, f32[256,256]{1,0:T(8,128)S(1)} %get-tuple-element.67), kind=kOutput, calls=%fused_computation.42 | convolution fusion | flops 1612185600 | bytes 4734976 | tf_op jit(solution)/shard_map/pij,pjk->pik/dot_general | solution.py:41
  175.8 3.3 multiply_reduce_fusion.5
  179.1 16.9 %copy.35 = f32[8,256,256]{0,2,1:T(8,128)} copy(f32[8,256,256]{1,2,0:T(8,128)S(1)} %get-tuple-element.58) | data formatting | bytes 4194304 | tf_op jit(solution)/shard_map/pji,pjk->pik/dot_general | solution.py:42
  196.0 2.3 gather_fusion.2
  200.1 5.1 %fusion.18 = f32[8,256,256]{1,2,0:T(8,128)S(1)} fusion(f32[8,256,256]{1,2,0:T(8,128)S(1)} %get-tuple-element.58, f32[8,256]{1,0:T(8,128)S(1)} %get-tuple-element.32, f32[256,256]{1,0:T(8,128)} %fusion.136, f32[8,256]{1,0:T(8,128)S(1)} %get-tuple-element.31, f32[256,256]{1,0:T(8,128)S(1)} %get-tuple-element.67), kind=kOutput, calls=%fused_computation.37 | convolution fusion | flops 1612185600 | bytes 4734976 | tf_op jit(solution)/shard_map/pij,pjk->pik/dot_general | solution.py:41
  205.2 3.3 multiply_reduce_fusion.4
  208.6 16.7 %copy.37 = f32[8,256,256]{0,2,1:T(8,128)} copy(f32[8,256,256]{1,2,0:T(8,128)S(1)} %get-tuple-element.60) | data formatting | bytes 4194304 | tf_op jit(solution)/shard_map/pji,pjk->pik/dot_general | solution.py:42
  225.3 2.3 gather_fusion.3
  228.3 4.1 fusion.19
  232.5 2.5 fusion.16
  235.3 2.5 fusion.13
  237.8 2.4 convolution_bitcast_fusion.1
  240.3 2.2 reshape.365
  245.2 5.0 %collective-permute-done = f32[64,8,128]{2,0,1:T(8,128)S(1)} collective-permute-done((f32[64,8,128]{2,0,1:T(8,128)S(1)}, f32[64,8,128]{2,0,1:T(8,128)S(1)}, u32[]{:S(2)}, u32[]{:S(2)}) %collective-permute-start) | collective-permute-done | bytes 262176 | tf_op jit(solution)/shard_map/ppermute | solution.py:12
  252.7 4.1 fusion.15
  256.8 7.4 %collective-permute-done.1 = f32[8,128,128]{1,2,0:T(8,128)S(1)} collective-permute-done((f32[8,128,128]{1,2,0:T(8,128)S(1)}, f32[8,128,128]{1,2,0:T(8,128)S(1)}, u32[]{:S(2)}, u32[]{:S(2)}) %collective-permute-start.1) | collective-permute-done | bytes 524320 | tf_op jit(solution)/shard_map/ppermute | solution.py:69
  265.4 2.6 fusion.14
  269.3 7.1 %collective-permute-done.2 = f32[8,128,128]{1,2,0:T(8,128)S(1)} collective-permute-done((f32[8,128,128]{1,2,0:T(8,128)S(1)}, f32[8,128,128]{1,2,0:T(8,128)S(1)}, u32[]{:S(2)}, u32[]{:S(2)}) %collective-permute-start.2) | collective-permute-done | bytes 524320 | tf_op jit(solution)/shard_map/ppermute | solution.py:69
  276.5 1.8 collective-permute-start.3
  280.1 19.8 %collective-permute-done.3 = f32[8,128,128]{1,2,0:T(8,128)S(1)} collective-permute-done((f32[8,128,128]{1,2,0:T(8,128)S(1)}, f32[8,128,128]{1,2,0:T(8,128)S(1)}, u32[]{:S(2)}, u32[]{:S(2)}) %collective-permute-start.3) | collective-permute-done | bytes 524320 | tf_op jit(solution)/shard_map/ppermute | solution.py:69
  303.6 16.6 %copy.45 = f32[8,256,256]{0,2,1:T(8,128)} copy(f32[8,256,256]{1,2,0:T(8,128)S(1)} %get-tuple-element.5) | data formatting | bytes 4194304 | tf_op jit(solution)/shard_map/concatenate | solution.py:75
  320.1 2.3 gather_fusion.4
  322.8 4.4 %fusion.12 = f32[8,256,256]{2,1,0:T(8,128)} fusion(f32[8,256]{1,0:T(8,128)S(1)} %get-tuple-element.28, f32[256,256]{1,0:T(8,128)} %fusion.138, f32[8,256]{1,0:T(8,128)S(1)} %get-tuple-element.27, f32[256,256]{1,0:T(8,128)S(1)} %get-tuple-element.67), kind=kOutput, calls=%fused_computation.27 | convolution fusion | flops 1612185600 | bytes 2637824 | tf_op jit(solution)/shard_map/pij,pjk->pik/dot_general | solution.py:43
  327.3 4.1 fusion.11
  331.4 2.8 multiply_reduce_fusion.2
  334.2 16.7 %copy.47 = f32[8,256,256]{0,2,1:T(8,128)} copy(f32[8,256,256]{1,2,0:T(8,128)S(1)} %get-tuple-element.62) | data formatting | bytes 4194304 | tf_op jit(solution)/shard_map/pji,pjk->pik/dot_general | solution.py:42
  350.9 2.3 gather_fusion.5
  353.6 4.1 fusion.8
  357.7 3.8 fusion.9
  361.4 2.7 multiply_reduce_fusion.1
  364.2 16.7 %copy.49 = f32[8,256,256]{0,2,1:T(8,128)} copy(f32[8,256,256]{1,2,0:T(8,128)S(1)} %get-tuple-element.64) | data formatting | bytes 4194304 | tf_op jit(solution)/shard_map/pji,pjk->pik/dot_general | solution.py:42
  380.9 2.3 gather_fusion.6
  383.6 4.1 fusion.5
  387.7 3.8 fusion.6
  391.5 2.7 multiply_reduce_fusion
  394.2 16.8 %copy.51 = f32[8,256,256]{0,2,1:T(8,128)} copy(f32[8,256,256]{1,2,0:T(8,128)S(1)} %get-tuple-element.66) | data formatting | bytes 4194304 | tf_op jit(solution)/shard_map/pji,pjk->pik/dot_general | solution.py:42
  411.0 2.3 gather_fusion.7
  413.7 4.1 fusion
  420.4 5.8 %collective-permute-done.5 = f32[64,8,128]{2,1,0:T(8,128)S(1)} collective-permute-done((f32[64,8,128]{2,1,0:T(8,128)S(1)}, f32[64,8,128]{2,1,0:T(8,128)S(1)}, u32[]{:S(2)}, u32[]{:S(2)}) %collective-permute-start.5) | collective-permute-done | bytes 262176 | tf_op jit(solution)/shard_map/ppermute | solution.py:12
  (164 shorter events, 37.9 us)
Async XLA Ops:
  6.5 109.9 %all-reduce.2.cloned.1.call-start = ((), (), s32[]{:S(2)}) async-start(), calls=%async_computation | async-start | bytes 4194304 | tf_op jit(solution)/shard_map/psum | solution.py:49
  8.0 3.3 copy-start.44
  11.3 122.9 %copy-start.32 = (s32[1,1,256]{2,1,0:T(1,128)}, s32[1,1,256]{2,1,0:T(1,128)S(1)}, u32[]{:S(2)}) copy-start(s32[1,1,256]{2,1,0:T(1,128)S(1)} %get-tuple-element.22) | copy-start | bytes 3076
  11.3 122.9 %copy-start.34 = (s32[1,1,256]{2,1,0:T(1,128)}, s32[1,1,256]{2,1,0:T(1,128)S(1)}, u32[]{:S(2)}) copy-start(s32[1,1,256]{2,1,0:T(1,128)S(1)} %get-tuple-element.16) | copy-start | bytes 3076
  11.3 122.8 %copy-start.36 = (s32[1,1,256]{2,1,0:T(1,128)}, s32[1,1,256]{2,1,0:T(1,128)S(1)}, u32[]{:S(2)}) copy-start(s32[1,1,256]{2,1,0:T(1,128)S(1)} %get-tuple-element.21) | copy-start | bytes 3076
  11.3 122.8 %copy-start.38 = (s32[1,1,256]{2,1,0:T(1,128)}, s32[1,1,256]{2,1,0:T(1,128)S(1)}, u32[]{:S(2)}) copy-start(s32[1,1,256]{2,1,0:T(1,128)S(1)} %get-tuple-element.20) | copy-start | bytes 3076
  11.3 122.8 %copy-start.40 = (s32[1,1,256]{2,1,0:T(1,128)}, s32[1,1,256]{2,1,0:T(1,128)S(1)}, u32[]{:S(2)}) copy-start(s32[1,1,256]{2,1,0:T(1,128)S(1)} %get-tuple-element.19) | copy-start | bytes 3076
  11.3 122.8 %copy-start.41 = (s32[1,1,256]{2,1,0:T(1,128)}, s32[1,1,256]{2,1,0:T(1,128)S(1)}, u32[]{:S(2)}) copy-start(s32[1,1,256]{2,1,0:T(1,128)S(1)} %get-tuple-element.18) | copy-start | bytes 3076
  11.3 122.8 %copy-start.42 = (s32[1,1,256]{2,1,0:T(1,128)}, s32[1,1,256]{2,1,0:T(1,128)S(1)}, u32[]{:S(2)}) copy-start(s32[1,1,256]{2,1,0:T(1,128)S(1)} %get-tuple-element.17) | copy-start | bytes 3076
  116.5 20.1 %copy-start = (f32[8,256,256]{2,1,0:T(8,128)S(1)}, f32[8,256,256]{2,1,0:T(8,128)}, u32[]{:S(2)}) copy-start(f32[8,256,256]{2,1,0:T(8,128)} %all-reduce.2.cloned.1.call-done) | copy-start | bytes 6291460
  142.5 4.1 copy-start.20
  170.6 5.1 %copy-start.25 = (f32[8,256]{1,0:T(8,128)}, f32[8,256]{1,0:T(8,128)S(1)}, u32[]{:S(2)}) copy-start(f32[8,256]{1,0:T(8,128)S(1)} %get-tuple-element.34) | copy-start | bytes 24580
  170.6 5.1 %copy-start.5 = (f32[256,256]{1,0:T(8,128)S(1)}, f32[256,256]{1,0:T(8,128)}, u32[]{:S(2)}) copy-start(f32[256,256]{1,0:T(8,128)} %fusion.135) | copy-start | bytes 786436
  170.6 5.1 %copy-start.19 = (f32[256,256]{0,1:T(8,128)S(1)}, f32[256,256]{0,1:T(8,128)}, u32[]{:S(2)}) copy-start(f32[256,256]{0,1:T(8,128)} %fusion.130) | copy-start | bytes 786436
  200.0 5.2 %copy-start.26 = (f32[8,256]{1,0:T(8,128)}, f32[8,256]{1,0:T(8,128)S(1)}, u32[]{:S(2)}) copy-start(f32[8,256]{1,0:T(8,128)S(1)} %get-tuple-element.31) | copy-start | bytes 24580
  200.0 5.2 %copy-start.28 = (f32[8,256]{1,0:T(8,128)}, f32[8,256]{1,0:T(8,128)S(1)}, u32[]{:S(2)}) copy-start(f32[8,256]{1,0:T(8,128)S(1)} %get-tuple-element.32) | copy-start | bytes 24580
  200.1 5.2 %copy-start.6 = (f32[256,256]{1,0:T(8,128)S(1)}, f32[256,256]{1,0:T(8,128)}, u32[]{:S(2)}) copy-start(f32[256,256]{1,0:T(8,128)} %fusion.136) | copy-start | bytes 786436
  200.1 5.2 %copy-start.18 = (f32[256,256]{0,1:T(8,128)S(1)}, f32[256,256]{0,1:T(8,128)}, u32[]{:S(2)}) copy-start(f32[256,256]{0,1:T(8,128)} %fusion.129) | copy-start | bytes 786436
  228.3 4.1 copy-start.7
  228.3 4.1 copy-start.27
  228.3 4.1 copy-start.29
  232.4 2.6 copy-start.30
  232.5 2.9 copy-start.3
  237.8 6.6 %copy-start.35 = (s32[1,1,256]{2,1,0:T(1,128)S(1)}, s32[1,1,256]{2,1,0:T(1,128)}, u32[]{:S(2)}) copy-start(s32[1,1,256]{2,1,0:T(1,128)} %copy-done.34) | copy-start | bytes 3076
  240.2 12.5 %copy-start.33 = (s32[1,1,256]{2,1,0:T(1,128)S(1)}, s32[1,1,256]{2,1,0:T(1,128)}, u32[]{:S(2)}) copy-start(s32[1,1,256]{2,1,0:T(1,128)} %copy-done.32) | copy-start | bytes 3076
  240.3 12.5 %copy-start.4 = (f32[256,256]{1,0:T(8,128)S(1)}, f32[256,256]{1,0:T(8,128)}, u32[]{:S(2)}) copy-start(f32[256,256]{1,0:T(8,128)} %fusion.137) | copy-start | bytes 786436
  240.3 12.5 %copy-start.24 = (f32[8,256]{1,0:T(8,128)S(1)}, f32[8,256]{1,0:T(8,128)}, u32[]{:S(2)}) copy-start(f32[8,256]{1,0:T(8,128)} %copy-done.23) | copy-start | bytes 24580
  244.1 6.1 %collective-permute-start = (f32[64,8,128]{2,0,1:T(8,128)S(1)}, f32[64,8,128]{2,0,1:T(8,128)S(1)}, u32[]{:S(2)}, u32[]{:S(2)}) collective-permute-start(f32[64,8,128]{2,0,1:T(8,128)S(1)} %bitcast.109), channel_id=1, source_target_pairs={{3,0},{0,1},{1,2},{2,3},{7,4},{4,5},{5,6},{6,7},{11,8},{8,9},{9,10... | collective-permute-start | bytes 786440 | tf_op jit(solution)/shard_map/ppermute | solution.py:12
  251.2 13.0 %collective-permute-start.1 = (f32[8,128,128]{1,2,0:T(8,128)S(1)}, f32[8,128,128]{1,2,0:T(8,128)S(1)}, u32[]{:S(2)}, u32[]{:S(2)}) collective-permute-start(f32[8,128,128]{1,2,0:T(8,128)S(1)} %fusion.194), channel_id=1, source_target_pairs={{0,4},{4,0},{8,12},{12,8},{16,20},{20,16},{24,28},{28,24},{1,5},{5... | collective-permute-start | bytes 1572872 | tf_op jit(solution)/shard_map/ppermute | solution.py:69
  264.3 12.1 %collective-permute-start.2 = (f32[8,128,128]{1,2,0:T(8,128)S(1)}, f32[8,128,128]{1,2,0:T(8,128)S(1)}, u32[]{:S(2)}, u32[]{:S(2)}) collective-permute-start(f32[8,128,128]{1,2,0:T(8,128)S(1)} %add.141), channel_id=1, source_target_pairs={{0,8},{4,12},{8,0},{12,4},{16,24},{20,28},{24,16},{28,20},{1,9},{5... | collective-permute-start | bytes 1572872 | tf_op jit(solution)/shard_map/ppermute | solution.py:69
  268.9 32.0 %collective-permute-start.4 = (f32[8,128,128]{1,2,0:T(8,128)S(1)}, f32[8,128,128]{1,2,0:T(8,128)S(1)}, u32[]{:S(2)}, u32[]{:S(2)}) collective-permute-start(f32[8,128,128]{1,2,0:T(8,128)S(1)} %get-tuple-element.8), channel_id=1, source_target_pairs={{3,0},{0,1},{1,2},{2,3},{7,4},{4,5},{5,6},{6,7},{11,8},{8,9},{9,10... | collective-permute-start | bytes 1572872 | tf_op jit(solution)/shard_map/ppermute | solution.py:12
  276.5 23.4 %collective-permute-start.3 = (f32[8,128,128]{1,2,0:T(8,128)S(1)}, f32[8,128,128]{1,2,0:T(8,128)S(1)}, u32[]{:S(2)}, u32[]{:S(2)}) collective-permute-start(f32[8,128,128]{1,2,0:T(8,128)S(1)} %add.142), channel_id=1, source_target_pairs={{0,16},{4,20},{8,24},{12,28},{16,0},{20,4},{24,8},{28,12},{1,17},{... | collective-permute-start | bytes 1572872 | tf_op jit(solution)/shard_map/ppermute | solution.py:69
  303.5 19.0 %copy-start.37 = (s32[1,1,256]{2,1,0:T(1,128)S(1)}, s32[1,1,256]{2,1,0:T(1,128)}, u32[]{:S(2)}) copy-start(s32[1,1,256]{2,1,0:T(1,128)} %copy-done.36) | copy-start | bytes 3076
  303.5 19.0 %copy-start.45 = (f32[256]{0:T(256)S(1)}, f32[256]{0:T(256)}, u32[]{:S(2)}) copy-start(f32[256]{0:T(256)} %get-tuple-element.43) | copy-start | bytes 3076
  303.5 19.0 %copy-start.46 = (f32[256]{0:T(256)S(1)}, f32[256]{0:T(256)}, u32[]{:S(2)}) copy-start(f32[256]{0:T(256)} %get-tuple-element.44) | copy-start | bytes 3076
  320.1 7.1 %copy-start.9 = (f32[256,256]{1,0:T(8,128)S(1)}, f32[256,256]{1,0:T(8,128)}, u32[]{:S(2)}) copy-start(f32[256,256]{1,0:T(8,128)} %fusion.138) | copy-start | bytes 786436
  320.1 7.1 %copy-start.11 = (f32[8,128,128]{1,2,0:T(8,128)S(1)}, f32[8,128,128]{1,2,0:T(8,128)}, u32[]{:S(2)}) copy-start(f32[8,128,128]{1,2,0:T(8,128)} %copy.44) | copy-start | bytes 1572868
  320.1 7.1 %copy-start.12 = (f32[8,128,128]{1,2,0:T(8,128)S(1)}, f32[8,128,128]{1,2,0:T(8,128)}, u32[]{:S(2)}) copy-start(f32[8,128,128]{1,2,0:T(8,128)} %get-tuple-element.7) | copy-start | bytes 1572868
  320.1 7.1 %copy-start.22 = (f32[8,128,128]{1,2,0:T(8,128)S(1)}, f32[8,128,128]{1,2,0:T(8,128)}, u32[]{:S(2)}) copy-start(f32[8,128,128]{1,2,0:T(8,128)} %copy-done.21) | copy-start | bytes 1572868
  327.2 4.1 copy-start.10
  327.3 4.1 copy-start.15
  353.6 4.1 copy-start.1
  357.7 3.8 copy-start.14
  383.6 4.1 copy-start.2
  387.7 3.8 copy-start.16
  394.2 19.5 %copy-start.17 = (f32[256,256]{1,0:T(8,128)S(1)}, f32[256,256]{1,0:T(8,128)}, u32[]{:S(2)}) copy-start(f32[256,256]{1,0:T(8,128)} %fusion.141) | copy-start | bytes 786436
  413.7 4.2 copy-start.13
  420.3 5.8 %collective-permute-start.5 = (f32[64,8,128]{2,1,0:T(8,128)S(1)}, f32[64,8,128]{2,1,0:T(8,128)S(1)}, u32[]{:S(2)}, u32[]{:S(2)}) collective-permute-start(f32[64,8,128]{2,1,0:T(8,128)S(1)} %bitcast.108), channel_id=1, source_target_pairs={{3,0},{0,1},{1,2},{2,3},{7,4},{4,5},{5,6},{6,7},{11,8},{8,9},{9,10... | collective-permute-start | bytes 786440 | tf_op jit(solution)/shard_map/ppermute | solution.py:12
  (8 other events, 17.4 us)
Sparse Core Ops, SparseCore 0:
  11.4 105.0 all-reduce.1
